TPU v7x, 32 devices: a whole 2x2x4 slice. The times are simulated.
32 devices in a mesh: dp: 4 (over y, core), expert: 4 (over z), tensor: 2 (over x).
Axes of the slice: x: 2, y: 2, z: 4, core: 2. Of those that a mesh axis runs over, the one named last changes fastest.
Arguments:
- tokens: bfloat16 [256, 3072], P(('dp', 'expert')), may hold values from -45 to 45
- cotangent: bfloat16 [256, 3072], P(('dp', 'expert')), may hold values from -6 to 6
- gain: float32 [3072], replicated, may hold values from 0.5 to 1.5
- w_router: bfloat16 [3072, 4], replicated, may hold values from -0.109375 to 0.109375
- w_gate: bfloat16 [4, 3072, 9216], P('expert', None, 'tensor'), may hold values from -0.109375 to 0.109375
- w_up: bfloat16 [4, 3072, 9216], P('expert', None, 'tensor'), may hold values from -0.109375 to 0.109375
- w_down: bfloat16 [4, 9216, 3072], P('expert', 'tensor'), may hold values from -0.0625 to 0.0625
- expert_ids: int32 [256, 2], P(('dp', 'expert')), may hold values from 0 to 3, as said below
- slots: int32 [256, 2], P(('dp', 'expert')), may hold values from 0 to 7, as said below
Outputs:
- mixed: bfloat16 [256, 3072], P(('dp', 'expert'))
- grad_tokens: bfloat16 [256, 3072], P(('dp', 'expert'))
- grad_router: float32 [3072, 4], replicated
- grad_gain: float32 [3072], replicated
Inputs may be any that keep to these rules, and one draw needn't show every extreme that they name: `expert_ids`: within each aligned block of 16 rows (one group), every expert is named exactly 8 times, and a row's two ids differ. Within each aligned block of 16 rows, the choices naming one expert hold its slots 0 to 7, each once.
All inputs are finite; a program needn't handle non-finite values.
Results may differ from a plain program's by a relative error of at most 0.0095.
Values may be sent and summed in bfloat16 or wider, within the bound.
A program may use at most 128 MiB of HBM per device.

v0:
```python
import jax
import jax.numpy as jnp
from jax import lax
from jax.sharding import PartitionSpec as P

epsilon = 1e-05


def pack_rows(select, values):
    return jnp.einsum("tcr,tcd->rd", select, values, preferred_element_type=jnp.float32).astype(
        jnp.bfloat16
    )


def repeat_blocks(packed, experts, copies):
    feature_width = packed.shape[1]
    blocks = packed.reshape(experts, 1, -1, feature_width)
    blocks = jnp.broadcast_to(blocks, (experts, copies, blocks.shape[2], feature_width))
    return blocks.reshape(experts * copies, -1, feature_width)


def to_experts(packed, experts, copies):
    arrived = lax.all_to_all(
        repeat_blocks(packed, experts, copies), "expert", split_axis=0, concat_axis=0, tiled=True
    )
    return arrived.reshape(-1, packed.shape[1])


def from_experts(partial_value, row_index, experts, copies):
    partial_value = lax.psum_scatter(
        partial_value.astype(jnp.bfloat16), "tensor", scatter_dimension=1, tiled=True
    ).astype(jnp.float32)
    feature_width = partial_value.shape[1]
    returned_rows = lax.all_to_all(
        partial_value.reshape(experts * copies, -1, feature_width),
        "expert",
        split_axis=0,
        concat_axis=0,
        tiled=True,
    )
    summed = jnp.sum(returned_rows.reshape(experts, copies, -1, feature_width), axis=1).reshape(
        -1, feature_width
    )
    picked = summed[row_index]
    picked = lax.all_gather(picked.astype(jnp.bfloat16), "tensor", axis=2, tiled=True).astype(
        picked.dtype
    )
    return picked


def shards(tokens, cotangent, gain, w_router, w_gate, w_up, w_down, expert_ids, slots):
    experts = w_router.shape[1]
    copies = lax.axis_size("expert") // experts
    token_count = tokens.shape[0]
    capacity = 2 * token_count // experts
    floats = tokens.astype(jnp.float32)
    inv_rms = lax.rsqrt(jnp.mean(floats * floats, axis=1, keepdims=True) + epsilon)
    normed = (floats * inv_rms * gain).astype(jnp.bfloat16)
    logits = jnp.dot(normed, w_router, preferred_element_type=jnp.float32)
    chosen_logits = jnp.take_along_axis(logits, expert_ids, axis=1)
    first_prob = jax.nn.sigmoid(chosen_logits[:, 0] - chosen_logits[:, 1])
    pair_probs = jnp.stack([first_prob, 1.0 - first_prob], axis=1)
    row_index = expert_ids * capacity + slots
    select = (
        row_index[:, :, None] == jnp.arange(experts * capacity, dtype=jnp.int32)[None, None, :]
    ).astype(jnp.bfloat16)
    feature_width = tokens.shape[1]
    inputs = to_experts(
        pack_rows(select, jnp.broadcast_to(normed[:, None, :], (token_count, 2, feature_width))),
        experts,
        copies,
    )
    gate_matrix = w_gate[0]
    up_matrix = w_up[0]
    down_matrix = w_down[0]
    gate_pre = jnp.dot(inputs, gate_matrix, preferred_element_type=jnp.float32)
    up_pre = jnp.dot(inputs, up_matrix, preferred_element_type=jnp.float32)
    activated = (jax.nn.silu(gate_pre) * up_pre).astype(jnp.bfloat16)
    chosen = from_experts(
        jnp.dot(activated, down_matrix, preferred_element_type=jnp.float32),
        row_index,
        experts,
        copies,
    )
    mixed = (floats + jnp.sum(pair_probs[:, :, None] * chosen, axis=1)).astype(jnp.bfloat16)
    upstream = cotangent.astype(jnp.float32)
    sent_grads = (pair_probs[:, :, None] * upstream[:, None, :]).astype(jnp.bfloat16)
    grad_outputs = to_experts(pack_rows(select, sent_grads), experts, copies)
    grad_act = jnp.dot(grad_outputs, down_matrix.T, preferred_element_type=jnp.float32)
    sigmoid_gate = jax.nn.sigmoid(gate_pre)
    grad_gate = (grad_act * up_pre * sigmoid_gate * (1.0 + gate_pre * (1.0 - sigmoid_gate))).astype(
        jnp.bfloat16
    )
    grad_up = (grad_act * jax.nn.silu(gate_pre)).astype(jnp.bfloat16)
    grad_inputs = jnp.dot(grad_gate, gate_matrix.T, preferred_element_type=jnp.float32) + jnp.dot(
        grad_up, up_matrix.T, preferred_element_type=jnp.float32
    )
    grad_mixture = jnp.sum(from_experts(grad_inputs, row_index, experts, copies), axis=1)
    grad_probs = jnp.sum(upstream[:, None, :] * chosen, axis=2)
    grad_first = first_prob * (1.0 - first_prob) * (grad_probs[:, 0] - grad_probs[:, 1])
    columns = jnp.arange(experts, dtype=jnp.int32)[None, :]
    grad_logits = grad_first[:, None] * (
        (expert_ids[:, 0:1] == columns).astype(jnp.float32)
        - (expert_ids[:, 1:2] == columns).astype(jnp.float32)
    )
    grad_normed = grad_mixture + jnp.dot(
        grad_logits, w_router.astype(jnp.float32).T, precision=lax.Precision.HIGHEST
    )
    router_part = jnp.dot(
        normed.astype(jnp.float32).T, grad_logits, precision=lax.Precision.HIGHEST
    )
    gain_part = jnp.sum(grad_normed * floats * inv_rms, axis=0)
    grad_router, grad_gain = lax.psum((router_part, gain_part), ("dp", "expert"))
    grad_scaled = grad_normed * gain
    cubed = inv_rms * inv_rms * inv_rms
    grad_tokens = (
        upstream
        + inv_rms * grad_scaled
        - floats * cubed * jnp.mean(grad_scaled * floats, axis=1, keepdims=True)
    ).astype(jnp.bfloat16)
    return (mixed, grad_tokens, grad_router, grad_gain)


def solution(mesh):
    return jax.shard_map(
        shards,
        mesh=mesh,
        in_specs=(
            P(("dp", "expert"), None),
            P(("dp", "expert"), None),
            P(),
            P(),
            P("expert", None, "tensor"),
            P("expert", None, "tensor"),
            P("expert", "tensor", None),
            P(("dp", "expert"), None),
            P(("dp", "expert"), None),
        ),
        out_specs=(P(("dp", "expert"), None), P(("dp", "expert"), None), P(), P()),
        check_vma=False,
    )
```

profile of v0, /device:TPU:0, one launch (start us, length us, event | category | flops | bytes accessed | tf_op | source)
XLA Modules:
  0.0 204.1 jit_solution(13842822642820997463)
XLA Ops:
  7.2 0.0 copy-start
  7.2 1.0 fusion.29
  8.2 0.7 compare_select_fusion
  8.9 1.0 fusion.31
  9.9 1.0 fusion.24
  10.9 6.3 %all-to-all-start = ((bf16[4,8,3072]{2,1,0:T(8,128)(2,1)}), bf16[4,8,3072]{2,1,0:T(8,128)(2,1)S(1)}, u32[]{:S(2)}, u32[]{:S(2)}) async-start(bf16[4,8,3072]{2,1,0:T(8,128)(2,1)} %fusion.24), calls=%async_computation | async-start | bytes 393216 | tf_op jit(solution)/shard_map/all_to_all | solution.py:23
  17.3 0.7 bitcast_or_fusion
  17.9 0.1 copy.39
  18.0 0.1 reshape.101
  18.1 0.0 copy-done
  18.1 0.1 fusion.59
  18.3 0.8 gather_fusion.2
  19.0 0.1 reshape.104
  19.1 0.1 copy.40
  19.2 0.7 and_select_fusion
  19.9 0.9 convert_element_type.70
  20.8 1.0 fusion.23
  21.8 2.9 %all-to-all-done = bf16[4,8,3072]{2,1,0:T(8,128)(2,1)S(1)} async-done(((bf16[4,8,3072]{2,1,0:T(8,128)(2,1)}), bf16[4,8,3072]{2,1,0:T(8,128)(2,1)S(1)}, u32[]{:S(2)}, u32[]{:S(2)}) %all-to-all-start) | async-done | bytes 196640 | tf_op jit(solution)/shard_map/all_to_all | solution.py:23
  24.8 3.4 %all-to-all-start.2 = ((bf16[4,8,3072]{2,1,0:T(8,128)(2,1)}), bf16[4,8,3072]{2,1,0:T(8,128)(2,1)S(1)}, u32[]{:S(2)}, u32[]{:S(2)}) async-start(bf16[4,8,3072]{2,1,0:T(8,128)(2,1)} %fusion.23), calls=%async_computation.3 | async-start | bytes 393216 | tf_op jit(solution)/shard_map/all_to_all | solution.py:23
  28.1 0.0 reduce-scatter.3.cloned.1.call-start
  28.2 11.5 %fusion.10 = f32[32,4608]{1,0:T(8,128)S(1)} fusion(bf16[1,3072,4608]{2,1,0:T(8,128)(2,1)} %param.13, bf16[4,8,3072]{2,1,0:T(8,128)(2,1)S(1)} %all-to-all-done), kind=kOutput, calls=%fused_computation.13 | convolution fusion | flops 905969664 | bytes 29097984 | tf_op jit(solution)/shard_map/dot_general | solution.py:76
  39.7 11.5 %fusion.6 = f32[32,4608]{1,0:T(8,128)S(1)} fusion(bf16[1,3072,4608]{2,1,0:T(8,128)(2,1)} %param.14, bf16[4,8,3072]{2,1,0:T(8,128)(2,1)S(1)} %all-to-all-done), kind=kOutput, calls=%fused_computation.9 | convolution fusion | flops 905969664 | bytes 29097984 | tf_op jit(solution)/shard_map/dot_general | solution.py:77
  51.2 12.3 %fusion.20 = bf16[32,3072]{1,0:T(8,128)(2,1)} fusion(bf16[1,4608,3072]{2,1,0:T(8,128)(2,1)} %param.15, f32[32,4608]{1,0:T(8,128)S(1)} %fusion.6, f32[32,4608]{1,0:T(8,128)S(1)} %fusion.10), kind=kOutput, calls=%fused_computation.21 | convolution fusion | flops 906952704 | bytes 29687808 | tf_op jit(solution)/shard_map/dot_general | solution.py:80
  63.6 0.0 reduce-scatter.3.cloned.1.call-update
  63.6 0.2 reduce-scatter.5.cloned.1.call-start
  63.8 0.0 all-to-all-done.2
  63.8 13.6 %fusion = f32[32,4608]{1,0:T(8,128)S(1)} fusion(bf16[1,4608,3072]{2,1,0:T(8,128)(2,1)} %param.15, bf16[4,8,3072]{2,1,0:T(8,128)(2,1)S(1)} %all-to-all-done.2), kind=kOutput, calls=%fused_computation.3 | convolution fusion | flops 905969664 | bytes 29097984 | tf_op jit(solution)/shard_map/dot_general | solution.py:89
  77.4 13.5 %fusion.4 = f32[32,3072]{1,0:T(8,128)S(1)} fusion(bf16[1,3072,4608]{2,1,0:T(8,128)(2,1)} %param.14, f32[32,4608]{1,0:T(8,128)S(1)} %fusion, f32[32,4608]{1,0:T(8,128)S(1)} %fusion.10), kind=kOutput, calls=%fused_computation.7 | convolution fusion | flops 906854400 | bytes 29884416 | tf_op jit(solution)/shard_map/dot_general | solution.py:95
  90.9 0.0 copy-start.4
  90.9 0.0 copy-start.1
  90.9 0.0 copy-start.3
  90.9 0.0 copy-start.2
  90.9 14.3 %fusion.15 = bf16[32,3072]{1,0:T(8,128)(2,1)} fusion(f32[32,3072]{1,0:T(8,128)S(1)} %fusion.4, bf16[1,3072,4608]{2,1,0:T(8,128)(2,1)} %param.13, f32[32,4608]{1,0:T(8,128)S(1)} %fusion.10, f32[32,4608]{1,0:T(8,128)S(1)} %fusion, f32[32,4608]{1,0:T(8,128)S(1)} %fusion.6), kind=kOutput, calls=%fused_computation.18 | convolution fusion | flops 907640832 | bytes 30670848 | tf_op jit(solution)/shard_map/dot_general | solution.py:95
  105.2 0.0 reduce-scatter.5.cloned.1.call-update
  105.2 0.0 reduce-scatter.3.cloned.1.call-done
  105.2 5.0 %all-to-all-start.1 = ((bf16[4,8,1536]{2,1,0:T(8,128)(2,1)}), bf16[4,8,1536]{2,1,0:T(8,128)(2,1)S(1)}, u32[]{:S(2)}, u32[]{:S(2)}) async-start(bf16[4,8,1536]{2,1,0:T(8,128)(2,1)} %bitcast.72), calls=%async_computation.2 | async-start | bytes 196608 | tf_op jit(solution)/shard_map/all_to_all | solution.py:34
  110.3 0.0 copy-done.4
  110.3 0.1 copy.41
  110.4 0.1 reshape.87
  110.5 7.3 %reduce-scatter.5.cloned.1.call-done = bf16[32,1536]{1,0:T(8,128)(2,1)} async-done(((bf16[32,3072]{1,0:T(8,128)(2,1)}), bf16[32,1536]{1,0:T(8,128)(2,1)}) %reduce-scatter.5.cloned.1.call-update) | async-done | bytes 98320 | tf_op jit(solution)/shard_map/reduce_scatter | solution.py:30
  117.8 0.0 all-to-all-done.1
  117.8 4.6 %all-to-all-start.3 = ((bf16[4,8,1536]{2,1,0:T(8,128)(2,1)}), bf16[4,8,1536]{2,1,0:T(8,128)(2,1)S(1)}, u32[]{:S(2)}, u32[]{:S(2)}) async-start(bf16[4,8,1536]{2,1,0:T(8,128)(2,1)} %bitcast.71), calls=%async_computation.5 | async-start | bytes 196608 | tf_op jit(solution)/shard_map/all_to_all | solution.py:34
  122.4 0.6 gather_fusion
  123.1 5.3 %all_gather.6 = bf16[16,2,3072]{2,0,1:T(8,128)(2,1)S(1)} all-gather(bf16[16,2,1536]{2,0,1:T(8,128)(2,1)S(1)} %copy.42), channel_id=1, replica_groups=mesh['dp'=4,'expert'=4,'tensor'=2] {'tensor'}, dimensions={2}, use_global_device_ids=true | all-gather | bytes 294912 | tf_op jit(solution)/shard_map/all_gather | solution.py:45
  128.4 0.1 fusion.27
  128.5 0.0 all-to-all-done.3
  128.5 0.6 gather_fusion.1
  129.2 5.3 %all_gather.7 = bf16[16,2,3072]{2,1,0:T(2,128)(2,1)S(1)} all-gather(bf16[16,2,1536]{2,1,0:T(2,128)(2,1)S(1)} %reshape.112), channel_id=1, replica_groups=mesh['dp'=4,'expert'=4,'tensor'=2] {'tensor'}, dimensions={2}, use_global_device_ids=true | all-gather | bytes 294912 | tf_op jit(solution)/shard_map/all_gather | solution.py:45
  134.5 0.5 convert_reduce_fusion
  135.0 0.3 fusion.47
  135.4 0.0 copy-done.1
  135.4 0.0 copy-done.3
  135.4 0.5 fusion.38
  135.8 60.6 %all-reduce = (f32[3072,4]{0,1:T(4,128)}, f32[3072]{0:T(1024)}) all-reduce(f32[3072,4]{0,1:T(4,128)S(1)} %fusion.47, f32[3072]{0:T(1024)S(1)} %get-tuple-element.4), channel_id=1, replica_groups=mesh['dp'=4,'expert'=4,'tensor'=2] {'dp','expert'}, use_global_device_ids=true, to_apply=%region_7.8 | all-reduce | flops 15360 | bytes 122880 | tf_op jit(solution)/shard_map/psum | solution.py:113
  196.5 0.0 copy-done.2
  196.5 0.8 fusion.35
  (10 shorter events, 0.2 us)
Async XLA Ops:
  7.2 11.0 %copy-start = (bf16[3072,4]{0,1:T(4,128)(2,1)S(1)}, bf16[3072,4]{0,1:T(4,128)(2,1)}, u32[]{:S(2)}) copy-start(bf16[3072,4]{0,1:T(4,128)(2,1)} %param.12) | copy-start | bytes 73732
  10.9 13.9 %all-to-all-start = ((bf16[4,8,3072]{2,1,0:T(8,128)(2,1)}), bf16[4,8,3072]{2,1,0:T(8,128)(2,1)S(1)}, u32[]{:S(2)}, u32[]{:S(2)}) async-start(bf16[4,8,3072]{2,1,0:T(8,128)(2,1)} %fusion.24), calls=%async_computation | async-start | bytes 393216 | tf_op jit(solution)/shard_map/all_to_all | solution.py:23
  24.8 39.0 %all-to-all-start.2 = ((bf16[4,8,3072]{2,1,0:T(8,128)(2,1)}), bf16[4,8,3072]{2,1,0:T(8,128)(2,1)S(1)}, u32[]{:S(2)}, u32[]{:S(2)}) async-start(bf16[4,8,3072]{2,1,0:T(8,128)(2,1)} %fusion.23), calls=%async_computation.3 | async-start | bytes 393216 | tf_op jit(solution)/shard_map/all_to_all | solution.py:23
  28.1 77.1 %reduce-scatter.3.cloned.1.call-start = ((), (), s32[]{:S(2)}) async-start(), calls=%async_computation.6 | async-start | bytes 294912 | tf_op jit(solution)/shard_map/reduce_scatter | solution.py:30
  63.6 54.2 %reduce-scatter.5.cloned.1.call-start = ((), (), s32[]{:S(2)}) async-start(), calls=%async_computation.7 | async-start | bytes 294912 | tf_op jit(solution)/shard_map/reduce_scatter | solution.py:30
  90.9 19.4 %copy-start.4 = (s32[16,2]{0,1:T(2,128)S(1)}, s32[16,2]{0,1:T(2,128)}, u32[]{:S(2)}) copy-start(s32[16,2]{0,1:T(2,128)} %param.16) | copy-start | bytes 388
  90.9 44.5 %copy-start.1 = (bf16[16,3072]{1,0:T(8,128)(2,1)S(1)}, bf16[16,3072]{1,0:T(8,128)(2,1)}, u32[]{:S(2)}) copy-start(bf16[16,3072]{1,0:T(8,128)(2,1)} %param.9) | copy-start | bytes 294916
  90.9 44.5 %copy-start.3 = (f32[3072]{0:T(1024)S(1)}, f32[3072]{0:T(1024)}, u32[]{:S(2)}) copy-start(f32[3072]{0:T(1024)} %param.11) | copy-start | bytes 36868
  90.9 105.5 %copy-start.2 = (bf16[16,3072]{1,0:T(8,128)(2,1)S(1)}, bf16[16,3072]{1,0:T(8,128)(2,1)}, u32[]{:S(2)}) copy-start(bf16[16,3072]{1,0:T(8,128)(2,1)} %param.10) | copy-start | bytes 294916
  105.2 12.5 %all-to-all-start.1 = ((bf16[4,8,1536]{2,1,0:T(8,128)(2,1)}), bf16[4,8,1536]{2,1,0:T(8,128)(2,1)S(1)}, u32[]{:S(2)}, u32[]{:S(2)}) async-start(bf16[4,8,1536]{2,1,0:T(8,128)(2,1)} %bitcast.72), calls=%async_computation.2 | async-start | bytes 196608 | tf_op jit(solution)/shard_map/all_to_all | solution.py:34
  117.8 10.8 %all-to-all-start.3 = ((bf16[4,8,1536]{2,1,0:T(8,128)(2,1)}), bf16[4,8,1536]{2,1,0:T(8,128)(2,1)S(1)}, u32[]{:S(2)}, u32[]{:S(2)}) async-start(bf16[4,8,1536]{2,1,0:T(8,128)(2,1)} %bitcast.71), calls=%async_computation.5 | async-start | bytes 196608 | tf_op jit(solution)/shard_map/all_to_all | solution.py:34
Sparse Core Ops, SparseCore 0:
  63.7 12.3 reduce-scatter.2
  105.3 12.3 reduce-scatter.4
where the time goes:
time: 205 us; the launch traced here: 204 us
  matrix products  79.6 us (39%)
  blocking collectives  71.2 us (35%)
  starting transfers between devices  19.6 us (10%)
  between operations  14.2 us (7%)
  waiting for transfers between devices  10.3 us (5%)
  other arithmetic  6.49 us (3%)
  local copies, waits for them, and re-layouts  2.68 us (1%)
    psum x1, blocking collectives, shards(): lax.psum((router_part, gain_part), ('dp', 'expert'))  60.6 us
    dot_general x1, matrix products, shards(): jnp.dot(grad_gate, gate_matrix.T, preferred_element_type=jnp.float32)  14.3 us
    dot_general x1, matrix products, shards(): jnp.dot(grad_outputs, down_matrix.T, preferred_element_type=jnp.float32)  13.6 us
    dot_general x1, matrix products, shards(): jnp.dot(grad_up, up_matrix.T, preferred_element_type=jnp.float32)  13.5 us
    dot_general x1, matrix products, shards(): jnp.dot(activated, down_matrix, preferred_element_type=jnp.float32)  12.3 us
    dot_general x1, matrix products, shards(): gate_pre = jnp.dot(inputs, gate_matrix, preferred_element_type=jnp.float32)  11.5 us
    dot_general x1, matrix products, shards(): up_pre = jnp.dot(inputs, up_matrix, preferred_element_type=jnp.float32)  11.5 us
    all_gather x2, blocking collectives, from_experts(): lax.all_gather(picked.astype(jnp.bfloat16), 'tensor', axis=2, tiled=True)  10.6 us
  transfers between devices with their start and end apart: 6, of which 2 were waited for; matrix products, arithmetic and copies ran while one was open for 40% of the time, Pallas kernels for 0%

commit v1 on v0

--- a/solution.py
+++ b/solution.py
@@ -1,6 +1,10 @@
+import functools
+
 import jax
 import jax.numpy as jnp
 from jax import lax
+from jax.experimental import pallas as pl
+from jax.experimental.pallas import tpu as pltpu
 from jax.sharding import PartitionSpec as P
 
 epsilon = 1e-05
@@ -121,9 +125,325 @@
     return (mixed, grad_tokens, grad_router, grad_gain)
 
 
+def nt_dot(rows, matrix):
+    return lax.dot_general(rows, matrix, (((1,), (1,)), ((), ())), preferred_element_type=jnp.float32)
+
+
+def tn_dot(left, right):
+    return lax.dot_general(left, right, (((0,), (0,)), ((), ())), preferred_element_type=jnp.float32)
+
+
+def layer_kernel(
+    E, NW, STEP,
+    tok, cot, gain, router, ids, slots, wg_any, wu_any, wd_any,
+    mixed_out, gtok_out, part_out,
+    wg, wu, wd, w_sem,
+    xsend, gsend, xbuf, gbuf, xs, gs,
+    x_s, x_r, g_s, g_r, xf_s, xf_r, gf_s, gf_r,
+    gate_s, up_s, act_s, gg_s, gu_s,
+    yown, ybf, yrecv, yret, ybuf, ym_s, ym_r, yz_s, yz_r,
+    iown, ibf, irecv, iret, ibuf, im_s, im_r, iz_s, iz_r,
+    mxown, mxrecv, gdown, gdrecv, gmown, gmrecv, tx_s, tx_r,
+):
+    dp = lax.axis_index("dp")
+    e = lax.axis_index("expert")
+    t = lax.axis_index("tensor")
+    c = lax.rem(dp, 2)
+    mate = {"dp": dp + 1 - 2 * c}
+    peer = {"tensor": 1 - t}
+    tokens, D = tok.shape
+    cap = xsend.shape[1]
+    half = wg.shape[1]
+    chunk = half // NW
+    started = []
+
+    def ahead(k):
+        return lax.rem(e + k, E)
+
+    def behind(k):
+        return lax.rem(e + E - k, E)
+
+    def send(src, dst, s, r, where):
+        copy = pltpu.make_async_remote_copy(
+            src_ref=src, dst_ref=dst, send_sem=s, recv_sem=r,
+            device_id=where, device_id_type=pl.DeviceIdType.MESH,
+        )
+        copy.start()
+        started.append(copy)
+        return copy
+
+    loads = []
+    for kind, (src, dst) in enumerate(((wg_any, wg), (wu_any, wu), (wd_any, wd))):
+        for i in range(NW):
+            begin = pl.multiple_of(c * half + i * chunk, 128)
+            here = pl.ds(i * chunk, chunk)
+            if kind < 2:
+                copy = pltpu.make_async_copy(
+                    src.at[0, :, pl.ds(begin, chunk)], dst.at[:, here], w_sem.at[kind, i]
+                )
+            else:
+                copy = pltpu.make_async_copy(
+                    src.at[0, pl.ds(begin, chunk), :], dst.at[here, :], w_sem.at[kind, i]
+                )
+            loads.append(copy)
+    for i in range(NW):
+        loads[i].start()
+        loads[NW + i].start()
+    for i in range(NW):
+        loads[2 * NW + i].start()
+
+    barrier = pltpu.get_barrier_semaphore()
+    for k in range(1, E):
+        pl.semaphore_signal(
+            barrier, inc=1, device_id={"expert": ahead(k)}, device_id_type=pl.DeviceIdType.MESH
+        )
+    pl.semaphore_signal(barrier, inc=1, device_id=mate, device_id_type=pl.DeviceIdType.MESH)
+    pl.semaphore_signal(barrier, inc=1, device_id=peer, device_id_type=pl.DeviceIdType.MESH)
+
+    floats = tok[...].astype(jnp.float32)
+    inv = lax.rsqrt(jnp.mean(floats * floats, axis=1, keepdims=True) + epsilon)
+    normed = (floats * inv * gain[...]).astype(jnp.bfloat16)
+    place = ids[...] * cap + slots[...]
+    lanes = lax.broadcasted_iota(jnp.int32, (tokens, E * cap), 1)
+    sel0 = (place[:, 0:1] == lanes).astype(jnp.float32)
+    sel1 = (place[:, 1:2] == lanes).astype(jnp.float32)
+    both = (sel0 + sel1).astype(jnp.bfloat16)
+    sel0 = sel0.astype(jnp.bfloat16)
+    sel1 = sel1.astype(jnp.bfloat16)
+    xsend[...] = tn_dot(both, normed).reshape(E, cap, D).astype(jnp.bfloat16)
+
+    pl.semaphore_wait(barrier, E + 1)
+
+    def dispatch(mine, buf, s, r, fs, fr):
+        copies = [
+            send(mine.at[ahead(k)], buf.at[c, e], s.at[k - 1], r.at[k - 1], {"expert": ahead(k)})
+            for k in range(1, E)
+        ]
+        forwards = [send(mine.at[e], buf.at[c, e], fs.at[0], fr.at[0], mate)]
+        buf[c, e] = mine[e]
+        return copies, forwards
+
+    def forward(copies, forwards, buf, fs, fr):
+        for k in range(1, E):
+            copies[k - 1].wait_recv()
+            spot = buf.at[c, behind(k)]
+            forwards.append(send(spot, spot, fs.at[k], fr.at[k], mate))
+
+    def arrive(forwards, buf, rows):
+        for copy in forwards:
+            copy.wait_recv()
+        rows[...] = buf[...].astype(jnp.float32).reshape(2 * E * cap, D).astype(jnp.bfloat16)
+
+    x_copies, x_forwards = dispatch(xsend, xbuf, x_s, x_r, xf_s, xf_r)
+
+    normed_f = normed.astype(jnp.float32)
+    first, second = ids[:, 0:1], ids[:, 1:2]
+    difference = jnp.zeros((tokens, 1), jnp.float32)
+    for j in range(E):
+        logit = jnp.sum(normed_f * router[j : j + 1, :].astype(jnp.float32), axis=1, keepdims=True)
+        difference += jnp.where(first == j, logit, 0.0) - jnp.where(second == j, logit, 0.0)
+    p0 = jax.nn.sigmoid(difference)
+    p1 = 1.0 - p0
+    upstream = cot[...].astype(jnp.float32)
+    gsend[...] = (
+        tn_dot(sel0, (p0 * upstream).astype(jnp.bfloat16))
+        + tn_dot(sel1, (p1 * upstream).astype(jnp.bfloat16))
+    ).reshape(E, cap, D).astype(jnp.bfloat16)
+    g_copies, g_forwards = dispatch(gsend, gbuf, g_s, g_r, gf_s, gf_r)
+
+    forward(x_copies, x_forwards, xbuf, xf_s, xf_r)
+    arrive(x_forwards, xbuf, xs)
+
+    per = chunk // STEP
+    for i in range(NW):
+        loads[i].wait()
+        loads[NW + i].wait()
+
+        @pl.loop(i * per, (i + 1) * per)
+        def _(n):
+            cols = pl.ds(pl.multiple_of(n * STEP, STEP), STEP)
+            g = jnp.dot(xs[...], wg[:, cols], preferred_element_type=jnp.float32)
+            u = jnp.dot(xs[...], wu[:, cols], preferred_element_type=jnp.float32)
+            gate_s[:, cols] = g
+            up_s[:, cols] = u
+            act_s[:, cols] = (jax.nn.silu(g) * u).astype(jnp.bfloat16)
+
+        if i == min(1, NW - 1):
+            forward(g_copies, g_forwards, gbuf, gf_s, gf_r)
+
+    for i in range(NW):
+        loads[2 * NW + i].wait()
+
+    @pl.loop(0, D // STEP)
+    def _(n):
+        cols = pl.ds(pl.multiple_of(n * STEP, STEP), STEP)
+        y = jnp.dot(act_s[...], wd[:, cols], preferred_element_type=jnp.float32)
+        y = y.reshape(2, E * cap, STEP)
+        yown[:, :, cols] = y
+        ybf[:, :, cols] = y.astype(jnp.bfloat16)
+
+    y_mate = send(ybf.at[1 - c], yrecv, ym_s, ym_r, mate)
+    arrive(g_forwards, gbuf, gs)
+
+    def give_back(own, arrived, ret, buf, s, r):
+        ret[...] = (own[c] + arrived[...].astype(jnp.float32)).reshape(E, cap, D).astype(jnp.bfloat16)
+        copies = [
+            send(ret.at[ahead(k)], buf.at[e], s.at[k - 1], r.at[k - 1], {"expert": ahead(k)})
+            for k in range(1, E)
+        ]
+        buf[e] = ret[e]
+        return copies
+
+    def back_rows(copies, buf):
+        for copy in copies:
+            copy.wait_recv()
+        return buf[...].astype(jnp.float32).reshape(E * cap, D).astype(jnp.bfloat16)
+
+    for i in range(NW):
+
+        @pl.loop(i * per, (i + 1) * per)
+        def _(n):
+            cols = pl.ds(pl.multiple_of(n * STEP, STEP), STEP)
+            grad_act = nt_dot(gs[...], wd[cols, :])
+            g = gate_s[:, cols]
+            sig = jax.nn.sigmoid(g)
+            gg_s[:, cols] = (grad_act * up_s[:, cols] * sig * (1.0 + g * (1.0 - sig))).astype(
+                jnp.bfloat16
+            )
+            gu_s[:, cols] = (grad_act * (g * sig)).astype(jnp.bfloat16)
+
+        if i == 0:
+            y_mate.wait_recv()
+            y_copies = give_back(yown, yrecv, yret, ybuf, yz_s, yz_r)
+
+    rows = back_rows(y_copies, ybuf)
+    chosen0 = jnp.dot(sel0, rows, preferred_element_type=jnp.float32)
+    chosen1 = jnp.dot(sel1, rows, preferred_element_type=jnp.float32)
+    mxown[...] = p0 * chosen0 + p1 * chosen1
+    gdown[...] = jnp.broadcast_to(
+        jnp.sum(upstream * (chosen0 - chosen1), axis=1, keepdims=True), gdown.shape
+    )
+    mx_copy = send(mxown, mxrecv, tx_s.at[0], tx_r.at[0], peer)
+    gd_copy = send(gdown, gdrecv, tx_s.at[1], tx_r.at[1], peer)
+
+    @pl.loop(0, D // STEP)
+    def _(n):
+        cols = pl.ds(pl.multiple_of(n * STEP, STEP), STEP)
+        back = nt_dot(gg_s[...], wg[cols, :]) + nt_dot(gu_s[...], wu[cols, :])
+        back = back.reshape(2, E * cap, STEP)
+        iown[:, :, cols] = back
+        ibf[:, :, cols] = back.astype(jnp.bfloat16)
+
+    i_mate = send(ibf.at[1 - c], irecv, im_s, im_r, mate)
+
+    mx_copy.wait_recv()
+    gd_copy.wait_recv()
+    mixed_out[...] = (floats + (mxown[...] + mxrecv[...])).astype(jnp.bfloat16)
+    grad_first = p0 * (1.0 - p0) * (gdown[:, 0:1] + gdrecv[:, 0:1])
+    part_out[...] = jnp.zeros_like(part_out)
+    through_router = jnp.zeros((tokens, D), jnp.float32)
+    for j in range(E):
+        grad_logit = grad_first * ((first == j).astype(jnp.float32) - (second == j).astype(jnp.float32))
+        through_router += grad_logit * router[j : j + 1, :].astype(jnp.float32)
+        part_out[j : j + 1, :] = jnp.sum(grad_logit * normed_f, axis=0, keepdims=True)
+
+    i_mate.wait_recv()
+    i_copies = give_back(iown, irecv, iret, ibuf, iz_s, iz_r)
+    rows = back_rows(i_copies, ibuf)
+    gmown[...] = jnp.dot(both, rows, preferred_element_type=jnp.float32).astype(jnp.bfloat16)
+    gm_copy = send(gmown, gmrecv, tx_s.at[2], tx_r.at[2], peer)
+    gm_copy.wait_recv()
+    grad_normed = (
+        gmown[...].astype(jnp.float32) + gmrecv[...].astype(jnp.float32)
+    ) + through_router
+    part_out[E : E + 1, :] = jnp.sum(grad_normed * floats * inv, axis=0, keepdims=True)
+    grad_scaled = grad_normed * gain[...]
+    gtok_out[...] = (
+        upstream
+        + inv * grad_scaled
+        - floats * (inv * inv * inv) * jnp.mean(grad_scaled * floats, axis=1, keepdims=True)
+    ).astype(jnp.bfloat16)
+    for copy in started:
+        copy.wait_send()
+
+
+def fused_shards(tokens, cotangent, gain, w_router, w_gate, w_up, w_down, expert_ids, slots):
+    E = w_router.shape[1]
+    count, D = tokens.shape
+    cap = 2 * count // E
+    half = w_gate.shape[2] // 2
+    rows = E * cap
+    bf, f32 = jnp.bfloat16, jnp.float32
+    STEP = 256
+    NW = 3 if half % (3 * STEP) == 0 else 1
+    vmem, dma = pltpu.VMEM, pltpu.SemaphoreType.DMA
+    whole = pl.BlockSpec(memory_space=pltpu.VMEM)
+    back = [
+        vmem((2, rows, D), f32), vmem((2, rows, D), bf), vmem((rows, D), bf),
+        vmem((E, cap, D), bf), vmem((E, cap, D), bf),
+        dma, dma, dma((E - 1,)), dma((E - 1,)),
+    ]
+    part_rows = -(-(E + 1) // 8) * 8
+    mixed, grad_tokens, part = pl.pallas_call(
+        functools.partial(layer_kernel, E, NW, STEP),
+        out_shape=(
+            jax.ShapeDtypeStruct((count, D), bf),
+            jax.ShapeDtypeStruct((count, D), bf),
+            jax.ShapeDtypeStruct((part_rows, D), f32),
+        ),
+        in_specs=[whole] * 6 + [pl.BlockSpec(memory_space=pl.ANY)] * 3,
+        out_specs=(whole,) * 3,
+        scratch_shapes=[
+            vmem((D, half), bf), vmem((D, half), bf), vmem((half, D), bf), dma((3, NW)),
+            vmem((E, cap, D), bf), vmem((E, cap, D), bf),
+            vmem((2, E, cap, D), bf), vmem((2, E, cap, D), bf),
+            vmem((2 * rows, D), bf), vmem((2 * rows, D), bf),
+            dma((E - 1,)), dma((E - 1,)), dma((E - 1,)), dma((E - 1,)),
+            dma((E,)), dma((E,)), dma((E,)), dma((E,)),
+            vmem((2 * rows, half), f32), vmem((2 * rows, half), f32),
+            vmem((2 * rows, half), bf), vmem((2 * rows, half), bf), vmem((2 * rows, half), bf),
+            *back, *back,
+            vmem((count, D), f32), vmem((count, D), f32),
+            vmem((count, 128), f32), vmem((count, 128), f32),
+            vmem((count, D), bf), vmem((count, D), bf),
+            dma((3,)), dma((3,)),
+        ],
+        compiler_params=pltpu.CompilerParams(
+            collective_id=0, has_side_effects=True, vmem_limit_bytes=63_000_000
+        ),
+    )(tokens, cotangent, gain[None, :], w_router.T, expert_ids, slots, w_gate, w_up, w_down)
+    summed = lax.psum(part, ("dp", "expert"))
+    return mixed, grad_tokens, summed[:E].T, summed[E]
+
+
+def fits(mesh):
+    return mesh.shape["dp"] % 2 == 0 and mesh.shape["tensor"] == 2 and mesh.shape["expert"] > 1
+
+
+def shards_for(mesh):
+    def body(*args):
+        experts = args[3].shape[1]
+        width, hidden = args[4].shape[1:]
+        count = args[0].shape[0]
+        cap = 2 * count // experts
+        weights = 3 * width * hidden
+        if (
+            fits(mesh)
+            and mesh.shape["expert"] == experts
+            and hidden % 512 == 0
+            and width % 256 == 0
+            and cap % 8 == 0
+            and weights <= 45_000_000
+        ):
+            return fused_shards(*args)
+        return shards(*args)
+
+    return body
+
+
 def solution(mesh):
     return jax.shard_map(
-        shards,
+        shards_for(mesh),
         mesh=mesh,
         in_specs=(
             P(("dp", "expert"), None),

time: 205 us -> 167 us (0.81)
  matrix products: 79.6 us -> 0 us
  waiting for transfers between devices: 10.3 us -> 87.7 us
  blocking collectives: 71.2 us -> 0 us
  Pallas kernels: 0 us -> 56.2 us
  starting transfers between devices: 19.6 us -> 0.04 us
  other arithmetic: 6.49 us -> 0 us
  local copies, waits for them, and re-layouts: 2.68 us -> 8.8 us
    psum x0 -> x1, waiting for transfers between devices: none -> 87.7 us  [fused_shards(): summed = lax.psum(part, ('dp', 'expert'))]
    dot_general x11 -> x0, matrix products: 79.6 us -> none  [the longest x1 14.3 us: shards(): jnp.dot(grad_gate, gate_matrix.T, preferred_element_type=jnp.float32)]
    psum x1 -> x0, blocking collectives: 60.6 us -> none  [shards(): lax.psum((router_part, gain_part), ('dp', 'expert'))]
    pallas_call x0 -> x1, Pallas kernels: none -> 56.2 us  [fused_shards(): pl.pallas_call(functools.partial(layer_kernel, E, NW, STEP), out_shape=(j...]
    all_to_all x4 -> x0, starting transfers between devices: 19.3 us -> none  [the longest x2 9.71 us: to_experts(): lax.all_to_all(repeat_blocks(packed, experts, copies), 'expert', split_ax...]
    all_gather x2 -> x0, blocking collectives: 10.6 us -> none  [from_experts(): lax.all_gather(picked.astype(jnp.bfloat16), 'tensor', axis=2, tiled=True)]
    reduce_scatter x2 -> x0, waiting for transfers between devices: 7.33 us -> none  [from_experts(): lax.psum_scatter(partial_value.astype(jnp.bfloat16), 'tensor', scatter_di...]
    unnamed x10 -> x4, local copies, waits for them, and re-layouts: 0.03 us -> 5.78 us
  transfers between devices with their start and end apart: 6 -> 1, of which waited for: 2 -> 1; matrix products, arithmetic and copies ran while one was open for 40% -> 0% of each run, Pallas kernels for 0% -> 0%
where the time goes in v1:
time: 167 us
  waiting for transfers between devices  87.7 us (53%)
  Pallas kernels  56.2 us (34%)
  between operations  14 us (8%)
  local copies, waits for them, and re-layouts  8.8 us (5%)
    psum x1, waiting for transfers between devices, fused_shards(): summed = lax.psum(part, ('dp', 'expert'))  87.7 us
    pallas_call x1, Pallas kernels, fused_shards(): pl.pallas_call(functools.partial(layer_kernel, E, NW, STEP), out_shape=(j...  56.2 us
    unnamed x4, local copies, waits for them, and re-layouts  5.78 us
  transfers between devices with their start and end apart: 1, of which 1 were waited for; matrix products, arithmetic and copies ran while one was open for 0% of the time, Pallas kernels for 0%

profile of v1, /device:TPU:0, one launch (start us, length us, event | category | flops | bytes accessed | tf_op | source)
XLA Modules:
  0.0 166.7 jit_solution(1860871401802147976)
XLA Ops:
  7.2 0.0 all-reduce.2.cloned.1.call-start
  7.2 1.4 copy.13.ids
  8.6 1.4 copy.14.slots
  9.9 56.2 %shard_map.120 = (bf16[16,3072]{1,0:T(8,128)(2,1)}, bf16[16,3072]{1,0:T(8,128)(2,1)}, f32[8,3072]{1,0:T(8,128)}) custom-call(bf16[16,3072]{1,0:T(8,128)(2,1)} %tok.1, bf16[16,3072]{1,0:T(8,128)(2,1)} %cot.1, f32[1,3072]{1,0:T(1,128)} %bitcast.6, bf16[4,3072]{1,0:T(4,128)(2,1)} %bitcast.5, s32[16,2]{1,0:T(8,128)} %copy.13.ids, s32[16,2]{1,0:T(8,128)} %copy.14.slots, ...), custom_call_target="tpu_custom_call" | custom-call | tf_op jit(solution)/shard_map/pallas_call | solution.py:387
  66.1 0.0 all-reduce.2.cloned.1.call-update
  66.1 87.7 %all-reduce.2.cloned.1.call-done = f32[8,3072]{1,0:T(8,128)} async-done(((f32[8,3072]{1,0:T(8,128)}), f32[8,3072]{1,0:T(8,128)}) %all-reduce.2.cloned.1.call-update) | async-done | bytes 98320 | tf_op jit(solution)/shard_map/psum | solution.py:415
  153.8 1.5 slice.9
  155.3 1.5 slice_bitcast_fusion
  156.8 1.5 copy.18
  158.3 1.5 copy.19
Async XLA Ops:
  7.2 146.6 %all-reduce.2.cloned.1.call-start = ((), (), s32[]{:S(2)}) async-start(), calls=%async_computation | async-start | bytes 196608 | tf_op jit(solution)/shard_map/psum | solution.py:415
Sparse Core Ops, SparseCore 0:
  66.2 87.4 all-reduce.1

commit v2 on v1

--- a/solution.py
+++ b/solution.py
@@ -134,7 +134,7 @@
 
 
 def layer_kernel(
-    E, NW, STEP,
+    E, NW, STEP, NP, groups,
     tok, cot, gain, router, ids, slots, wg_any, wu_any, wd_any,
     mixed_out, gtok_out, part_out,
     wg, wu, wd, w_sem,
@@ -144,6 +144,7 @@
     yown, ybf, yrecv, yret, ybuf, ym_s, ym_r, yz_s, yz_r,
     iown, ibf, irecv, iret, ibuf, im_s, im_r, iz_s, iz_r,
     mxown, mxrecv, gdown, gdrecv, gmown, gmrecv, tx_s, tx_r,
+    blocks, inbox, outbox, rs_s, rs_r, ag_s, ag_r,
 ):
     dp = lax.axis_index("dp")
     e = lax.axis_index("expert")
@@ -193,26 +194,31 @@
         loads[2 * NW + i].start()
 
     barrier = pltpu.get_barrier_semaphore()
-    for k in range(1, E):
+    rank = dp * E + e
+
+    def member(k):
+        other = lax.rem(rank + k, groups)
+        return other, {"dp": other // E, "expert": lax.rem(other, E)}
+
+    for k in range(1, groups):
         pl.semaphore_signal(
-            barrier, inc=1, device_id={"expert": ahead(k)}, device_id_type=pl.DeviceIdType.MESH
+            barrier, inc=1, device_id=member(k)[1], device_id_type=pl.DeviceIdType.MESH
         )
-    pl.semaphore_signal(barrier, inc=1, device_id=mate, device_id_type=pl.DeviceIdType.MESH)
     pl.semaphore_signal(barrier, inc=1, device_id=peer, device_id_type=pl.DeviceIdType.MESH)
 
     floats = tok[...].astype(jnp.float32)
     inv = lax.rsqrt(jnp.mean(floats * floats, axis=1, keepdims=True) + epsilon)
     normed = (floats * inv * gain[...]).astype(jnp.bfloat16)
     place = ids[...] * cap + slots[...]
-    lanes = lax.broadcasted_iota(jnp.int32, (tokens, E * cap), 1)
-    sel0 = (place[:, 0:1] == lanes).astype(jnp.float32)
-    sel1 = (place[:, 1:2] == lanes).astype(jnp.float32)
+    index = lax.broadcasted_iota(jnp.int32, (E * cap, tokens), 0)
+    sel0 = (place[0:1, :] == index).astype(jnp.float32)
+    sel1 = (place[1:2, :] == index).astype(jnp.float32)
     both = (sel0 + sel1).astype(jnp.bfloat16)
     sel0 = sel0.astype(jnp.bfloat16)
     sel1 = sel1.astype(jnp.bfloat16)
-    xsend[...] = tn_dot(both, normed).reshape(E, cap, D).astype(jnp.bfloat16)
-
-    pl.semaphore_wait(barrier, E + 1)
+    xsend[...] = jnp.dot(both, normed, preferred_element_type=jnp.float32).reshape(E, cap, D).astype(jnp.bfloat16)
+
+    pl.semaphore_wait(barrier, groups)
 
     def dispatch(mine, buf, s, r, fs, fr):
         copies = [
@@ -237,7 +243,14 @@
     x_copies, x_forwards = dispatch(xsend, xbuf, x_s, x_r, xf_s, xf_r)
 
     normed_f = normed.astype(jnp.float32)
-    first, second = ids[:, 0:1], ids[:, 1:2]
+    diagonal = lax.broadcasted_iota(jnp.int32, (tokens, tokens), 0) == lax.broadcasted_iota(
+        jnp.int32, (tokens, tokens), 1
+    )
+
+    def as_column(row):
+        return jnp.sum(jnp.where(diagonal, row.astype(jnp.float32), 0.0), axis=1, keepdims=True)
+
+    first, second = as_column(ids[0:1, :]), as_column(ids[1:2, :])
     difference = jnp.zeros((tokens, 1), jnp.float32)
     for j in range(E):
         logit = jnp.sum(normed_f * router[j : j + 1, :].astype(jnp.float32), axis=1, keepdims=True)
@@ -246,8 +259,8 @@
     p1 = 1.0 - p0
     upstream = cot[...].astype(jnp.float32)
     gsend[...] = (
-        tn_dot(sel0, (p0 * upstream).astype(jnp.bfloat16))
-        + tn_dot(sel1, (p1 * upstream).astype(jnp.bfloat16))
+        jnp.dot(sel0, (p0 * upstream).astype(jnp.bfloat16), preferred_element_type=jnp.float32)
+        + jnp.dot(sel1, (p1 * upstream).astype(jnp.bfloat16), preferred_element_type=jnp.float32)
     ).reshape(E, cap, D).astype(jnp.bfloat16)
     g_copies, g_forwards = dispatch(gsend, gbuf, g_s, g_r, gf_s, gf_r)
 
@@ -282,16 +295,25 @@
         yown[:, :, cols] = y
         ybf[:, :, cols] = y.astype(jnp.bfloat16)
 
-    y_mate = send(ybf.at[1 - c], yrecv, ym_s, ym_r, mate)
+    y_mate = send(ybf.at[1 - c], yrecv, ym_s.at[0], ym_r.at[0], mate)
     arrive(g_forwards, gbuf, gs)
 
-    def give_back(own, arrived, ret, buf, s, r):
-        ret[...] = (own[c] + arrived[...].astype(jnp.float32)).reshape(E, cap, D).astype(jnp.bfloat16)
+    def give_back(own, arrived, ret, buf, s, r, part, width):
+        at = pl.ds(part * width, width)
+        ret[:, :, at] = (own[c, :, at] + arrived[:, at].astype(jnp.float32)).reshape(
+            E, cap, width
+        ).astype(jnp.bfloat16)
         copies = [
-            send(ret.at[ahead(k)], buf.at[e], s.at[k - 1], r.at[k - 1], {"expert": ahead(k)})
+            send(
+                ret.at[ahead(k), :, at],
+                buf.at[e, :, at],
+                s.at[part, k - 1],
+                r.at[part, k - 1],
+                {"expert": ahead(k)},
+            )
             for k in range(1, E)
         ]
-        buf[e] = ret[e]
+        buf[e, :, at] = ret[e, :, at]
         return copies
 
     def back_rows(copies, buf):
@@ -314,11 +336,11 @@
 
         if i == 0:
             y_mate.wait_recv()
-            y_copies = give_back(yown, yrecv, yret, ybuf, yz_s, yz_r)
+            y_copies = give_back(yown, yrecv, yret, ybuf, yz_s, yz_r, 0, D)
 
     rows = back_rows(y_copies, ybuf)
-    chosen0 = jnp.dot(sel0, rows, preferred_element_type=jnp.float32)
-    chosen1 = jnp.dot(sel1, rows, preferred_element_type=jnp.float32)
+    chosen0 = tn_dot(sel0, rows)
+    chosen1 = tn_dot(sel1, rows)
     mxown[...] = p0 * chosen0 + p1 * chosen1
     gdown[...] = jnp.broadcast_to(
         jnp.sum(upstream * (chosen0 - chosen1), axis=1, keepdims=True), gdown.shape
@@ -326,48 +348,93 @@
     mx_copy = send(mxown, mxrecv, tx_s.at[0], tx_r.at[0], peer)
     gd_copy = send(gdown, gdrecv, tx_s.at[1], tx_r.at[1], peer)
 
-    @pl.loop(0, D // STEP)
-    def _(n):
-        cols = pl.ds(pl.multiple_of(n * STEP, STEP), STEP)
-        back = nt_dot(gg_s[...], wg[cols, :]) + nt_dot(gu_s[...], wu[cols, :])
-        back = back.reshape(2, E * cap, STEP)
-        iown[:, :, cols] = back
-        ibf[:, :, cols] = back.astype(jnp.bfloat16)
-
-    i_mate = send(ibf.at[1 - c], irecv, im_s, im_r, mate)
+    width = D // NP
+    i_mates, i_copies = [], []
+
+    def reduce_part(part):
+        i_mates[part].wait_recv()
+        i_copies.extend(give_back(iown, irecv, iret, ibuf, iz_s, iz_r, part, width))
+
+    for part in range(NP):
+
+        @pl.loop(part * (width // STEP), (part + 1) * (width // STEP))
+        def _(n):
+            cols = pl.ds(pl.multiple_of(n * STEP, STEP), STEP)
+            back = nt_dot(gg_s[...], wg[cols, :]) + nt_dot(gu_s[...], wu[cols, :])
+            back = back.reshape(2, E * cap, STEP)
+            iown[:, :, cols] = back
+            ibf[:, :, cols] = back.astype(jnp.bfloat16)
+
+        at = pl.ds(part * width, width)
+        i_mates.append(
+            send(ibf.at[1 - c, :, at], irecv.at[:, at], im_s.at[part], im_r.at[part], mate)
+        )
+        if part > 0:
+            reduce_part(part - 1)
+    reduce_part(NP - 1)
 
     mx_copy.wait_recv()
     gd_copy.wait_recv()
     mixed_out[...] = (floats + (mxown[...] + mxrecv[...])).astype(jnp.bfloat16)
     grad_first = p0 * (1.0 - p0) * (gdown[:, 0:1] + gdrecv[:, 0:1])
-    part_out[...] = jnp.zeros_like(part_out)
     through_router = jnp.zeros((tokens, D), jnp.float32)
+    sums = []
     for j in range(E):
         grad_logit = grad_first * ((first == j).astype(jnp.float32) - (second == j).astype(jnp.float32))
         through_router += grad_logit * router[j : j + 1, :].astype(jnp.float32)
-        part_out[j : j + 1, :] = jnp.sum(grad_logit * normed_f, axis=0, keepdims=True)
-
-    i_mate.wait_recv()
-    i_copies = give_back(iown, irecv, iret, ibuf, iz_s, iz_r)
+        sums.append(jnp.sum(grad_logit * normed_f, axis=0, keepdims=True))
+
     rows = back_rows(i_copies, ibuf)
-    gmown[...] = jnp.dot(both, rows, preferred_element_type=jnp.float32).astype(jnp.bfloat16)
+    gmown[...] = tn_dot(both, rows).astype(jnp.bfloat16)
     gm_copy = send(gmown, gmrecv, tx_s.at[2], tx_r.at[2], peer)
     gm_copy.wait_recv()
     grad_normed = (
         gmown[...].astype(jnp.float32) + gmrecv[...].astype(jnp.float32)
     ) + through_router
-    part_out[E : E + 1, :] = jnp.sum(grad_normed * floats * inv, axis=0, keepdims=True)
+    sums.append(jnp.sum(grad_normed * floats * inv, axis=0, keepdims=True))
+    piece = blocks.shape[2]
+    blocks[...] = jnp.zeros_like(blocks)
+    for j, row in enumerate(sums):
+        for k in range(groups):
+            blocks[k, j : j + 1, :] = row[:, k * piece : (k + 1) * piece]
+    shares = []
+    for k in range(1, groups):
+        other, where = member(k)
+        shares.append(send(blocks.at[other], inbox.at[rank], rs_s.at[k - 1], rs_r.at[k - 1], where))
+    inbox[rank] = blocks[rank]
     grad_scaled = grad_normed * gain[...]
     gtok_out[...] = (
         upstream
         + inv * grad_scaled
         - floats * (inv * inv * inv) * jnp.mean(grad_scaled * floats, axis=1, keepdims=True)
     ).astype(jnp.bfloat16)
+    for copy in shares:
+        copy.wait_recv()
+    total = inbox[0]
+    for k in range(1, groups):
+        total += inbox[k]
+    outbox[rank] = total
+    shares = []
+    for k in range(1, groups):
+        shares.append(
+            send(outbox.at[rank], outbox.at[rank], ag_s.at[k - 1], ag_r.at[k - 1], member(k)[1])
+        )
+    for copy in shares:
+        copy.wait_recv()
+    for k in range(groups):
+        part_out[:, k * piece : (k + 1) * piece] = outbox[k]
     for copy in started:
         copy.wait_send()
 
 
-def fused_shards(tokens, cotangent, gain, w_router, w_gate, w_up, w_down, expert_ids, slots):
+def unpack_kernel(E, mixed, gtok, part, mixed_out, gtok_out, router_out, gain_out):
+    mixed_out[...] = mixed[...]
+    gtok_out[...] = gtok[...]
+    router_out[...] = part[0:E, :]
+    gain_out[...] = part[E : E + 1, :]
+
+
+def fused_shards(groups, tokens, cotangent, gain, w_router, w_gate, w_up, w_down, expert_ids, slots):
     E = w_router.shape[1]
     count, D = tokens.shape
     cap = 2 * count // E
@@ -376,16 +443,17 @@
     bf, f32 = jnp.bfloat16, jnp.float32
     STEP = 256
     NW = 3 if half % (3 * STEP) == 0 else 1
+    NP = 3 if D % (3 * STEP) == 0 else 1
     vmem, dma = pltpu.VMEM, pltpu.SemaphoreType.DMA
     whole = pl.BlockSpec(memory_space=pltpu.VMEM)
     back = [
         vmem((2, rows, D), f32), vmem((2, rows, D), bf), vmem((rows, D), bf),
         vmem((E, cap, D), bf), vmem((E, cap, D), bf),
-        dma, dma, dma((E - 1,)), dma((E - 1,)),
+        dma((NP,)), dma((NP,)), dma((NP, E - 1)), dma((NP, E - 1)),
     ]
     part_rows = -(-(E + 1) // 8) * 8
     mixed, grad_tokens, part = pl.pallas_call(
-        functools.partial(layer_kernel, E, NW, STEP),
+        functools.partial(layer_kernel, E, NW, STEP, NP, groups),
         out_shape=(
             jax.ShapeDtypeStruct((count, D), bf),
             jax.ShapeDtypeStruct((count, D), bf),
@@ -407,13 +475,25 @@
             vmem((count, 128), f32), vmem((count, 128), f32),
             vmem((count, D), bf), vmem((count, D), bf),
             dma((3,)), dma((3,)),
+            *[vmem((groups, part_rows, D // groups), f32)] * 3,
+            *[dma((groups - 1,))] * 4,
         ],
         compiler_params=pltpu.CompilerParams(
             collective_id=0, has_side_effects=True, vmem_limit_bytes=63_000_000
         ),
-    )(tokens, cotangent, gain[None, :], w_router.T, expert_ids, slots, w_gate, w_up, w_down)
-    summed = lax.psum(part, ("dp", "expert"))
-    return mixed, grad_tokens, summed[:E].T, summed[E]
+    )(tokens, cotangent, gain[None, :], w_router.T, expert_ids.T, slots.T, w_gate, w_up, w_down)
+    mixed, grad_tokens, router, gain = pl.pallas_call(
+        functools.partial(unpack_kernel, E),
+        out_shape=(
+            jax.ShapeDtypeStruct((count, D), bf),
+            jax.ShapeDtypeStruct((count, D), bf),
+            jax.ShapeDtypeStruct((E, D), f32),
+            jax.ShapeDtypeStruct((1, D), f32),
+        ),
+        in_specs=[whole] * 3,
+        out_specs=(whole,) * 4,
+    )(mixed, grad_tokens, part)
+    return mixed, grad_tokens, router.T, gain[0]
 
 
 def fits(mesh):
@@ -433,9 +513,10 @@
             and hidden % 512 == 0
             and width % 256 == 0
             and cap % 8 == 0
+            and width % (mesh.shape["dp"] * experts) == 0
             and weights <= 45_000_000
         ):
-            return fused_shards(*args)
+            return fused_shards(mesh.shape["dp"] * experts, *args)
         return shards(*args)
 
     return body

time: 167 us -> 68.2 us (0.41)
  waiting for transfers between devices: 87.7 us -> 0 us
  between operations: 14 us -> 0.64 us
  Pallas kernels: 56.2 us -> 67.4 us
  local copies, waits for them, and re-layouts: 8.8 us -> 0 us
    psum x1 -> x0, waiting for transfers between devices: 87.7 us -> none  [fused_shards(): summed = lax.psum(part, ('dp', 'expert'))]
    pallas_call x1 -> x2, Pallas kernels: 56.2 us -> 67.4 us  [the longest x1 65.7 us: fused_shards(): pl.pallas_call(functools.partial(layer_kernel, E, NW, STEP, NP, groups),...]
    unnamed x4 -> x0, local copies, waits for them, and re-layouts: 5.78 us -> none
  transfers between devices with their start and end apart: 1 -> 0, of which waited for: 1 -> 0; matrix products, arithmetic and copies ran while one was open for 0% -> 0% of each run, Pallas kernels for 0% -> 0%
where the time goes in v2:
time: 68.2 us; the launch traced here: 68.1 us
  Pallas kernels  67.4 us (99%)
    pallas_call x1, Pallas kernels, fused_shards(): pl.pallas_call(functools.partial(layer_kernel, E, NW, STEP, NP, groups),...  65.7 us
    pallas_call x1, Pallas kernels, fused_shards(): pl.pallas_call(functools.partial(unpack_kernel, E), out_shape=(jax.ShapeD...  1.68 us

profile of v2, /device:TPU:0, one launch (start us, length us, event | category | flops | bytes accessed | tf_op | source)
XLA Modules:
  0.0 68.1 jit_solution(17270304139031431708)
XLA Ops:
  0.6 65.7 %shard_map.120 = (bf16[16,3072]{1,0:T(8,128)(2,1)}, bf16[16,3072]{1,0:T(8,128)(2,1)}, f32[8,3072]{1,0:T(8,128)}) custom-call(bf16[16,3072]{1,0:T(8,128)(2,1)} %tok.1, bf16[16,3072]{1,0:T(8,128)(2,1)} %cot.1, f32[1,3072]{1,0:T(1,128)} %bitcast.7, bf16[4,3072]{1,0:T(4,128)(2,1)} %bitcast.6, s32[2,16]{1,0:T(2,128)} %bitcast.8, s32[2,16]{1,0:T(2,128)} %bitcast.9, ...), custom_call_target="tpu_custom_call" | custom-call | tf_op jit(solution)/shard_map/pallas_call | solution.py:455
  66.4 1.7 %shard_map.121 = (bf16[16,3072]{1,0:T(8,128)(2,1)}, bf16[16,3072]{1,0:T(8,128)(2,1)}, f32[4,3072]{1,0:T(4,128)}, f32[1,3072]{1,0:T(1,128)}) custom-call(bf16[16,3072]{1,0:T(8,128)(2,1)} %get-tuple-element.11.mixed, bf16[16,3072]{1,0:T(8,128)(2,1)} %get-tuple-element.12.gtok, f32[8,3072]{1,0:T(8,128)} %get-tuple-element.13.part), custom_call_target="tpu_custom_call" | custom-call | tf_op jit(solution)/shard_map/pallas_call | solution.py:485
